TPU v7x, 32 devices: a whole 2x2x4 slice. The times are simulated.
32 devices in a mesh: dp: 16 (over z, x, core), tensor: 2 (over y).
Axes of the slice: x: 2, y: 2, z: 4, core: 2. Of those that a mesh axis runs over, the one named last changes fastest.
Arguments:
- block_input: bfloat16 [32, 577, 1024], P('dp'), may hold values from -6 to 6
- first_scale: float32 [1024], replicated, may hold values from 0.5 to 1.5
- first_shift: float32 [1024], replicated, may hold values from -3 to 3
- heads_weight: bfloat16 [1024, 3, 1024], P(None, None, 'tensor'), may hold values from -0.1875 to 0.1875
- heads_bias: float32 [2, 1024], P(None, 'tensor'), may hold values from -3 to 3
- mixing_weight: bfloat16 [1024, 1024], P('tensor'), may hold values from -0.75 to 0.75
- mixing_bias: float32 [1024], replicated, may hold values from -3 to 3
- second_scale: float32 [1024], replicated, may hold values from 0.5 to 1.5
- second_shift: float32 [1024], replicated, may hold values from -3 to 3
- expand_weight: bfloat16 [1024, 4096], P(None, 'tensor'), may hold values from -0.1875 to 0.1875
- expand_bias: float32 [4096], P('tensor'), may hold values from -3 to 3
- shrink_weight: bfloat16 [4096, 1024], P('tensor'), may hold values from -0.09375 to 0.09375
- shrink_bias: float32 [1024], replicated, may hold values from -3 to 3
- output_grad: bfloat16 [32, 577, 1024], P('dp'), may hold values from -6 to 6
Outputs:
- block_output: bfloat16 [32, 577, 1024], P('dp')
- input_grad: bfloat16 [32, 577, 1024], P('dp')
- heads_weight_grad: float32 [1024, 3, 1024], P(None, None, 'tensor')
- heads_bias_grad: float32 [2, 1024], P(None, 'tensor')
- mixing_weight_grad: float32 [1024, 1024], P('tensor')
- mixing_bias_grad: float32 [1024], replicated
- second_scale_grad: float32 [1024], replicated
- second_shift_grad: float32 [1024], replicated
- expand_weight_grad: float32 [1024, 4096], P(None, 'tensor')
- expand_bias_grad: float32 [4096], P('tensor')
- shrink_weight_grad: float32 [4096, 1024], P('tensor')
- shrink_bias_grad: float32 [1024], replicated
- first_scale_grad: float32 [1024], replicated
- first_shift_grad: float32 [1024], replicated
All inputs are finite; a program needn't handle non-finite values.
Results may differ from a plain program's by a relative error of at most 0.012.
Values sent between devices are 32-bit elements; how exact they have to be, the bound alone decides.
A program may use at most 256 MiB of HBM per device.

v0:
```python
import math
import jax
import jax.numpy as jnp
from jax import lax
from jax.sharding import PartitionSpec as P

HEAD_DIM = 64
EPSILON = 1e-06


def normalize(values):
    center = values - jnp.mean(values, axis=-1, keepdims=True)
    inverse = lax.rsqrt(jnp.mean(center * center, axis=-1, keepdims=True) + EPSILON)
    return (center * inverse, inverse)


def norm_back(grad_out, scale, normed, inverse):
    scaled = grad_out * scale
    return inverse * (
        scaled
        - jnp.mean(scaled, axis=-1, keepdims=True)
        - normed * jnp.mean(scaled * normed, axis=-1, keepdims=True)
    )


def gelu_slope(pre_act):
    cumul = 0.5 * (1.0 + lax.erf(pre_act * 0.7071067811865476))
    return cumul + pre_act * jnp.exp(-0.5 * pre_act * pre_act) * 0.3989422804014327


def cross_dot(left_side, right_side):
    return lax.dot_general(
        left_side, right_side, (((0,), (0,)), ((), ())), preferred_element_type=jnp.float32
    )


def back_dot(left_side, right_side):
    return lax.dot_general(
        left_side, right_side, (((1,), (1,)), ((), ())), preferred_element_type=jnp.float32
    )


def on_device(
    block_input,
    first_scale,
    first_shift,
    heads_weight,
    heads_bias,
    mixing_weight,
    mixing_bias,
    second_scale,
    second_shift,
    expand_weight,
    expand_bias,
    shrink_weight,
    shrink_bias,
    output_grad,
):
    images, length, width = block_input.shape
    local = heads_weight.shape[2]
    heads_here = local // HEAD_DIM
    total_rows = images * length
    factor = 1.0 / math.sqrt(HEAD_DIM)
    head_shape = (images, length, heads_here, HEAD_DIM)
    flat_in = block_input.reshape(total_rows, width).astype(jnp.float32)
    normed_one, inverse_one = normalize(flat_in)
    layer_one = (normed_one * first_scale + first_shift).astype(jnp.bfloat16)
    joined_weight = heads_weight.reshape(width, 3 * local)
    projected = jnp.dot(layer_one, joined_weight, preferred_element_type=jnp.float32).reshape(
        total_rows, 3, local
    )
    queries = (projected[:, 0] + heads_bias[0]).astype(jnp.bfloat16).reshape(head_shape)
    keys_all = projected[:, 1].astype(jnp.bfloat16).reshape(head_shape)
    values_all = (projected[:, 2] + heads_bias[1]).astype(jnp.bfloat16).reshape(head_shape)
    scores = (
        jnp.einsum("bqhd,bkhd->bhqk", queries, keys_all, preferred_element_type=jnp.float32)
        * factor
    )
    logsum = jax.nn.logsumexp(scores, axis=-1, keepdims=True)
    probs_low = jnp.exp(scores - logsum).astype(jnp.bfloat16)
    attended = jnp.einsum(
        "bhqk,bkhd->bqhd", probs_low, values_all, preferred_element_type=jnp.float32
    )
    attended = attended.astype(jnp.bfloat16).reshape(total_rows, local)
    mixed = lax.psum(jnp.dot(attended, mixing_weight, preferred_element_type=jnp.float32), "tensor")
    hidden_one = flat_in + mixed + mixing_bias
    normed_two, inverse_two = normalize(hidden_one)
    layer_two = (normed_two * second_scale + second_shift).astype(jnp.bfloat16)
    pre_act = jnp.dot(layer_two, expand_weight, preferred_element_type=jnp.float32) + expand_bias
    activated = jax.nn.gelu(pre_act, approximate=False).astype(jnp.bfloat16)
    shrunk = lax.psum(
        jnp.dot(activated, shrink_weight, preferred_element_type=jnp.float32), "tensor"
    )
    block_output = (
        (hidden_one + shrunk + shrink_bias).astype(jnp.bfloat16).reshape(images, length, width)
    )
    owner = lax.axis_index("tensor")
    share = images // lax.axis_size("tensor")

    def own_sum(rows_wide):
        picked = lax.dynamic_slice_in_dim(
            rows_wide.reshape(images, length, width), owner * share, share, 0
        )
        return jnp.sum(picked, axis=(0, 1))

    upstream = output_grad.reshape(total_rows, width)
    upstream_wide = upstream.astype(jnp.float32)
    shrink_grad = cross_dot(activated, upstream)
    shrink_bias_part = own_sum(upstream_wide)
    pre_grad = back_dot(upstream, shrink_weight) * gelu_slope(pre_act)
    pre_low = pre_grad.astype(jnp.bfloat16)
    expand_bias_grad = jnp.sum(pre_grad, axis=0)
    expand_grad = cross_dot(layer_two, pre_low)
    partial_two = back_dot(pre_low, expand_weight)
    second_scale_part = jnp.sum(partial_two * normed_two, axis=0)
    second_shift_part = jnp.sum(partial_two, axis=0)
    layer_two_grad = lax.psum(partial_two, "tensor")
    hidden_grad = upstream_wide + norm_back(layer_two_grad, second_scale, normed_two, inverse_two)
    mixing_bias_part = own_sum(hidden_grad)
    hidden_low = hidden_grad.astype(jnp.bfloat16)
    mixing_grad = cross_dot(attended, hidden_low)
    attended_grad = back_dot(hidden_low, mixing_weight).astype(jnp.bfloat16).reshape(head_shape)
    scores = (
        jnp.einsum("bqhd,bkhd->bhqk", queries, keys_all, preferred_element_type=jnp.float32)
        * factor
    )
    probs = jnp.exp(scores - logsum)
    values_grad = jnp.einsum(
        "bhqk,bqhd->bkhd",
        probs.astype(jnp.bfloat16),
        attended_grad,
        preferred_element_type=jnp.float32,
    )
    probs_grad = jnp.einsum(
        "bqhd,bkhd->bhqk", attended_grad, values_all, preferred_element_type=jnp.float32
    )
    row_dot = jnp.sum(probs * probs_grad, axis=-1, keepdims=True)
    score_low = (probs * (probs_grad - row_dot) * factor).astype(jnp.bfloat16)
    queries_grad = jnp.einsum(
        "bhqk,bkhd->bqhd", score_low, keys_all, preferred_element_type=jnp.float32
    )
    keys_grad = jnp.einsum(
        "bhqk,bqhd->bkhd", score_low, queries, preferred_element_type=jnp.float32
    )
    stacked = jnp.stack(
        [
            queries_grad.reshape(total_rows, local),
            keys_grad.reshape(total_rows, local),
            values_grad.reshape(total_rows, local),
        ],
        axis=1,
    )
    heads_bias_grad = jnp.stack([jnp.sum(stacked[:, 0], axis=0), jnp.sum(stacked[:, 2], axis=0)])
    stacked_low = stacked.astype(jnp.bfloat16).reshape(total_rows, 3 * local)
    heads_grad = cross_dot(layer_one, stacked_low).reshape(width, 3, local)
    partial_one = back_dot(stacked_low, joined_weight)
    first_scale_part = jnp.sum(partial_one * normed_one, axis=0)
    first_shift_part = jnp.sum(partial_one, axis=0)
    layer_one_grad = lax.psum(partial_one, "tensor")
    input_grad = hidden_grad + norm_back(layer_one_grad, first_scale, normed_one, inverse_one)
    input_grad = input_grad.astype(jnp.bfloat16).reshape(images, length, width)
    bias_heads_sum, bias_expand_sum = lax.psum((heads_bias_grad, expand_bias_grad), "dp")
    (
        first_scale_sum,
        first_shift_sum,
        second_scale_sum,
        second_shift_sum,
        mixing_bias_sum,
        shrink_bias_sum,
    ) = lax.psum(
        (
            first_scale_part,
            first_shift_part,
            second_scale_part,
            second_shift_part,
            mixing_bias_part,
            shrink_bias_part,
        ),
        ("dp", "tensor"),
    )
    weight_part = (
        lax.psum_scatter(heads_grad, "dp", scatter_dimension=0, tiled=True),
        lax.psum_scatter(mixing_grad, "dp", scatter_dimension=0, tiled=True),
        lax.psum_scatter(expand_grad, "dp", scatter_dimension=0, tiled=True),
        lax.psum_scatter(shrink_grad, "dp", scatter_dimension=0, tiled=True),
    )
    heads_full, mixing_full, expand_full, shrink_full = (
        lax.all_gather(weight_part[0], "dp", axis=0, tiled=True),
        lax.all_gather(weight_part[1], "dp", axis=0, tiled=True),
        lax.all_gather(weight_part[2], "dp", axis=0, tiled=True),
        lax.all_gather(weight_part[3], "dp", axis=0, tiled=True),
    )
    return (
        block_output,
        input_grad,
        heads_full,
        bias_heads_sum,
        mixing_full,
        mixing_bias_sum,
        second_scale_sum,
        second_shift_sum,
        expand_full,
        bias_expand_sum,
        shrink_full,
        shrink_bias_sum,
        first_scale_sum,
        first_shift_sum,
    )


def solution(mesh):
    placed = (
        P("dp", None, None),
        P(),
        P(),
        P(None, None, "tensor"),
        P(None, "tensor"),
        P("tensor", None),
        P(),
        P(),
        P(),
        P(None, "tensor"),
        P("tensor"),
        P("tensor", None),
        P(),
        P("dp", None, None),
    )
    return jax.shard_map(
        on_device,
        mesh=mesh,
        in_specs=placed,
        out_specs=(
            P("dp", None, None),
            P("dp", None, None),
            P(None, None, "tensor"),
            P(None, "tensor"),
            P("tensor", None),
            P(),
            P(),
            P(),
            P(None, "tensor"),
            P("tensor"),
            P("tensor", None),
            P(),
            P(),
            P(),
        ),
        check_vma=False,
    )
```

profile of v0, /device:TPU:0, one launch (start us, length us, event | category | flops | bytes accessed | tf_op | source)
XLA Modules:
  0.0 1360.8 jit_solution(9283532576933548809)
XLA Ops:
  30.2 6.5 fusion.29
  45.1 5.1 copy.118
  58.6 14.0 %multiply_reduce_fusion.1 = (f32[2,8,577]{2,1,0:T(8,128)S(1)}, f32[2,8,577,577]{2,3,1,0:T(8,128)}) fusion(bf16[2,577,8,64]{1,3,2,0:T(8,128)(2,1)} %copy.120, f32[2,577,8,64]{1,3,2,0:T(8,128)} %copy.118, f32[8,64]{1,0:T(8,128)S(1)} %add.150), kind=kOutput, calls=%fused_computation.6 | convolution fusion | flops 693664768 | bytes 24891520 | tf_op jit(solution)/shard_map/bqhd,bkhd->bhqk/dot_general | solution.py:76
  72.6 10.4 exponential_reduce_fusion
  94.7 12.8 fusion.48
  132.0 110.1 %all-reduce.7.cloned.1.call-done = f32[1154,1024]{1,0:T(8,128)} async-done(((f32[1154,1024]{1,0:T(8,128)}), f32[1154,1024]{1,0:T(8,128)}) %all-reduce.7.cloned.1.call-update) | async-done | bytes 4726800 | tf_op jit(solution)/shard_map/psum | solution.py:85
  250.5 28.3 %fusion.7 = (bf16[1154,2048]{1,0:T(8,128)(2,1)}, f32[1154,2048]{1,0:T(8,128)}) fusion(f32[2048]{0:T(1024)S(1)} %copy-done.44, bf16[1024,2048]{1,0:T(8,128)(2,1)S(1)} %copy-done.42, f32[1154,1024]{1,0:T(8,128)S(1)} %get-tuple-element.91, f32[1024]{0:T(1024)S(1)} %copy-done.45, f32[1024]{0:T(1024)S(1)} %copy-done.35, f32[1154]{0:T(1024)S(1)} %add_rsqrt_fusion.1, ...), kind=kOutput, calls=%fused_computation.14 | convolution fusion | flops 5002119168 | bytes 23127056 | tf_op jit(solution)/shard_map/dot_general | solution.py:89
  278.7 10.9 fusion.69
  291.9 6.8 fusion.33
  298.7 120.1 %all-reduce.9.cloned.1.call-done = f32[1154,1024]{1,0:T(8,128)} async-done(((f32[1154,1024]{1,0:T(8,128)}), f32[1154,1024]{1,0:T(8,128)}) %all-reduce.9.cloned.1.call-update) | async-done | bytes 4726800 | tf_op jit(solution)/shard_map/psum | solution.py:117
  418.8 7.2 multiply_reduce_fusion.3
  441.3 13.8 %fusion.72 = f32[2,8,577,577]{2,3,1,0:T(8,128)} fusion(bf16[2,577,8,64]{1,3,2,0:T(8,128)(2,1)} %copy.125, bf16[2,577,8,64]{1,3,2,0:T(8,128)(2,1)S(1)} %copy-done.8), kind=kOutput, calls=%fused_computation.107 | convolution fusion | flops 681838592 | bytes 23670848 | tf_op jit(solution)/shard_map/bqhd,bkhd->bhqk/dot_general | solution.py:134
  455.2 27.6 %fusion.66 = (f32[8,64]{1,0:T(8,128)S(1)}, bf16[2,577,8,64]{1,3,2,0:T(8,128)(2,1)}) fusion(bf16[2,577,8,64]{1,3,2,0:T(8,128)(2,1)} %copy.120, f32[2,8,577,577]{2,3,1,0:T(8,128)} %fusion.72, f32[2,8,577]{2,1,0:T(8,128)S(1)} %copy-done.26, f32[2,8,577,577]{2,3,1,0:T(8,128)} %get-tuple-element.95, bf16[2,577,8,64]{1,3,2,0:T(8,128)(2,1)} %copy.125, ...), kind=kOutput, calls=%fused_computation.103 | convolution fusion | flops 1412809728 | bytes 47380672 | tf_op jit(solution)/shard_map/bhqk,bkhd->bqhd/dot_general | solution.py:139
  491.0 27.1 %fusion.39 = bf16[2,577,8,64]{1,3,2,0:T(8,128)(2,1)} fusion(f32[2,8,577,577]{2,3,1,0:T(8,128)} %fusion.72, f32[2,8,577]{2,1,0:T(8,128)S(1)} %copy-done.26, f32[2,8,577,577]{2,3,1,0:T(8,128)} %get-tuple-element.95, bf16[2,577,8,64]{1,3,2,0:T(8,128)(2,1)} %copy.125, bf16[2,577,8,64]{1,3,2,0:T(8,128)(2,1)S(1)} %copy-done.8, f32[2,577,8,64]{1,3,2,0:T(8,128)} %copy.118, ...), kind=kOutput, calls=%fused_computation.72 | convolution fusion | flops 1412810240 | bytes 48562368 | tf_op jit(solution)/shard_map/bhqk,bqhd->bkhd/dot_general | solution.py:142
  526.3 11.1 fusion.65
  543.9 9.7 fusion.27
  554.3 11.4 fusion.31
  567.6 10.6 fusion.73
  579.1 10.1 fusion.71
  589.2 5.7 convolution_bitcast_fusion
  594.9 44.0 %reduce-scatter.5.cloned.1.call-done = f32[64,3,512]{2,0,1:T(8,128)} async-done(((f32[1024,3,512]{2,0,1:T(8,128)}), f32[64,3,512]{2,0,1:T(8,128)}) %reduce-scatter.5.cloned.1.call-update) | async-done | bytes 393232 | tf_op jit(solution)/shard_map/reduce_scatter | solution.py:182
  639.0 107.1 %reduce-scatter.9.cloned.1.call-done = f32[64,2048]{1,0:T(8,128)} async-done(((f32[1024,2048]{1,0:T(8,128)}), f32[64,2048]{1,0:T(8,128)}) %reduce-scatter.9.cloned.1.call-update) | async-done | bytes 524304 | tf_op jit(solution)/shard_map/reduce_scatter | solution.py:184
  746.1 107.5 %reduce-scatter.11.cloned.1.call-done = f32[128,1024]{1,0:T(8,128)} async-done(((f32[2048,1024]{1,0:T(8,128)}), f32[128,1024]{1,0:T(8,128)}) %reduce-scatter.11.cloned.1.call-update) | async-done | bytes 524304 | tf_op jit(solution)/shard_map/reduce_scatter | solution.py:185
  857.3 5.1 reshape.211
  862.6 60.9 %all-reduce.1 = (f32[2,512]{1,0:T(2,128)}, f32[2048]{0:T(1024)}) all-reduce(f32[2,512]{1,0:T(2,128)S(1)} %pad_maximum_fusion, f32[2048]{0:T(1024)S(1)} %copy-done.37), channel_id=1, replica_groups=mesh['dp'=16,'tensor'=2] {'dp'}, use_global_device_ids=true, to_apply=%region_18.0 | all-reduce | flops 3072 | bytes 24576 | tf_op jit(solution)/shard_map/psum | solution.py:162
  925.5 195.1 %all-reduce.11.cloned.1.call-done = (f32[1154,1024]{1,0:T(8,128)}, f32[1154,1024]{1,0:T(8,128)}) async-done(((f32[1154,1024]{1,0:T(8,128)}, f32[1154,1024]{1,0:T(8,128)}), (f32[1154,1024]{1,0:T(8,128)}, f32[1154,1024]{1,0:T(8,128)})) %all-reduce.11.cloned.1.call-update) | async-done | bytes 9453584 | tf_op jit(solution)/shard_map/psum | solution.py:91
  1120.6 6.4 multiply_reduce_fusion.2
  1138.8 5.0 add_convert_fusion.1
  1149.8 42.4 %all-reduce = (f32[1024]{0:T(1024)}, f32[1024]{0:T(1024)}, f32[1024]{0:T(1024)}, f32[1024]{0:T(1024)}, f32[1024]{0:T(1024)}, /*index=5*/f32[1024]{0:T(1024)}) all-reduce(f32[1024]{0:T(1024)S(1)} %dynamic-slice_reduce_fusion, f32[1024]{0:T(1024)S(1)} %copy-done.33, ...), channel_id=1, replica_groups=mesh['dp'=16,'tensor'=2] {'dp','tensor'}, use_global_device_ids=true, to_apply=%region_21.0 | all-reduce | flops 6144 | bytes 49152 | tf_op jit(solution)/shard_map/psum | solution.py:170
  1192.2 69.0 %all-gather.9.cloned.1.call-done = f32[1024,2048]{1,0:T(8,128)} async-done(((f32[64,2048]{1,0:T(8,128)}), f32[1024,2048]{1,0:T(8,128)}) %all-gather.9.cloned.1.call-update) | async-done | bytes 8388624 | tf_op jit(solution)/shard_map/all_gather | solution.py:190
  1261.2 75.1 %all-gather.11.cloned.1.call-done = f32[2048,1024]{1,0:T(8,128)} async-done(((f32[128,1024]{1,0:T(8,128)}), f32[2048,1024]{1,0:T(8,128)}) %all-gather.11.cloned.1.call-update) | async-done | bytes 8388624 | tf_op jit(solution)/shard_map/all_gather | solution.py:191
  1336.3 6.9 copy.172
  (194 shorter events, 162.3 us)
Async XLA Ops:
  7.2 107.1 %copy-start = (bf16[512,1024]{1,0:T(8,128)(2,1)S(1)}, bf16[512,1024]{1,0:T(8,128)(2,1)}, u32[]{:S(2)}) copy-start(bf16[512,1024]{1,0:T(8,128)(2,1)} %param.19) | copy-start | bytes 3145732
  7.2 234.9 %all-reduce.7.cloned.1.call-start = ((), (), s32[]{:S(2)}) async-start(), calls=%async_computation.4 | async-start | bytes 9502720 | tf_op jit(solution)/shard_map/psum | solution.py:85
  58.6 14.0 %copy-start.29 = (f32[8,64]{1,0:T(8,128)}, f32[8,64]{1,0:T(8,128)S(1)}, u32[]{:S(2)}) copy-start(f32[8,64]{1,0:T(8,128)S(1)} %add.150) | copy-start | bytes 6148
  83.0 11.6 copy-start.25
  94.7 12.8 copy-start.7
  119.3 299.5 %all-reduce.9.cloned.1.call-start = ((), (), s32[]{:S(2)}) async-start(), calls=%async_computation.5 | async-start | bytes 9502720 | tf_op jit(solution)/shard_map/psum | solution.py:117
  127.4 114.8 %copy-start.38 = (f32[1024]{0:T(1024)S(1)}, f32[1024]{0:T(1024)}, u32[]{:S(2)}) copy-start(f32[1024]{0:T(1024)} %param.20) | copy-start | bytes 12292
  246.5 32.2 %copy-start.2 = (f32[1154,1024]{1,0:T(8,128)}, f32[1154,1024]{1,0:T(8,128)S(1)}, u32[]{:S(2)}) copy-start(f32[1154,1024]{1,0:T(8,128)S(1)} %get-tuple-element.91) | copy-start | bytes 14180356
  250.4 175.5 %copy-start.27 = (f32[1154]{0:T(1024)}, f32[1154]{0:T(1024)S(1)}, u32[]{:S(2)}) copy-start(f32[1154]{0:T(1024)S(1)} %add_rsqrt_fusion.1) | copy-start | bytes 13852
  250.4 28.3 %copy-start.10 = (bf16[1154,1024]{1,0:T(8,128)(2,1)S(1)}, bf16[1154,1024]{1,0:T(8,128)(2,1)}, u32[]{:S(2)}) copy-start(bf16[1154,1024]{1,0:T(8,128)(2,1)} %reshape.208) | copy-start | bytes 7090180
  250.4 28.3 %copy-start.43 = (bf16[2048,1024]{1,0:T(8,128)(2,1)S(1)}, bf16[2048,1024]{1,0:T(8,128)(2,1)}, u32[]{:S(2)}) copy-start(bf16[2048,1024]{1,0:T(8,128)(2,1)} %param.25) | copy-start | bytes 12582916
  298.7 279.7 %reduce-scatter.7.cloned.1.call-start = ((), (), s32[]{:S(2)}) async-start(), calls=%async_computation.8 | async-start | bytes 2228224 | tf_op jit(solution)/shard_map/reduce_scatter | solution.py:183
  441.3 13.9 %copy-start.26 = (f32[2,8,577]{2,1,0:T(8,128)S(1)}, f32[2,8,577]{2,1,0:T(8,128)}, u32[]{:S(2)}) copy-start(f32[2,8,577]{2,1,0:T(8,128)} %copy-done.25) | copy-start | bytes 110788
  441.3 197.6 %reduce-scatter.5.cloned.1.call-start = ((), (), s32[]{:S(2)}) async-start(), calls=%async_computation.6 | async-start | bytes 6684672 | tf_op jit(solution)/shard_map/reduce_scatter | solution.py:182
  553.6 192.4 %reduce-scatter.9.cloned.1.call-start = ((), (), s32[]{:S(2)}) async-start(), calls=%async_computation.10 | async-start | bytes 8912896 | tf_op jit(solution)/shard_map/reduce_scatter | solution.py:184
  565.8 287.9 %reduce-scatter.11.cloned.1.call-start = ((), (), s32[]{:S(2)}) async-start(), calls=%async_computation.12 | async-start | bytes 8912896 | tf_op jit(solution)/shard_map/reduce_scatter | solution.py:185
  578.3 347.2 %all-gather.7.cloned.1.call-start = ((), (), s32[]{:S(2)}) async-start(), calls=%async_computation.9 | async-start | bytes 2228224 | tf_op jit(solution)/shard_map/all_gather | solution.py:189
  579.0 10.2 copy-start.22
  579.0 10.2 copy-start.23
  579.0 541.6 %all-reduce.11.cloned.1.call-start = ((), (), s32[]{:S(2)}) async-start(), calls=%async_computation.14 | async-start | bytes 19005440 | tf_op jit(solution)/shard_map/psum | solution.py:91
  579.1 10.1 copy-start.18
  579.1 10.1 copy-start.24
  594.9 258.8 %copy-start.20 = (f32[2,577]{0,1:T(8,128)S(1)}, f32[2,577]{0,1:T(8,128)}, u32[]{:S(2)}) copy-start(f32[2,577]{0,1:T(8,128)} %copy-done.19) | copy-start | bytes 13852
  594.9 259.0 %copy-start.16 = (f32[2,577]{0,1:T(8,128)S(1)}, f32[2,577]{0,1:T(8,128)}, u32[]{:S(2)}) copy-start(f32[2,577]{0,1:T(8,128)} %copy-done.15) | copy-start | bytes 13852
  594.9 259.3 %copy-start.12 = (bf16[2,577,1024]{2,0,1:T(2,128)(2,1)S(1)}, bf16[2,577,1024]{2,0,1:T(2,128)(2,1)}, u32[]{:S(2)}) copy-start(bf16[2,577,1024]{2,0,1:T(2,128)(2,1)} %param.27) | copy-start | bytes 7090180
  594.9 597.3 %all-gather.5.cloned.1.call-start = ((), (), s32[]{:S(2)}) async-start(), calls=%async_computation.7 | async-start | bytes 6684672 | tf_op jit(solution)/shard_map/all_gather | solution.py:188
  639.0 622.2 %all-gather.9.cloned.1.call-start = ((), (), s32[]{:S(2)}) async-start(), calls=%async_computation.11 | async-start | bytes 8912896 | tf_op jit(solution)/shard_map/all_gather | solution.py:190
  746.1 590.2 %all-gather.11.cloned.1.call-start = ((), (), s32[]{:S(2)}) async-start(), calls=%async_computation.13 | async-start | bytes 8912896 | tf_op jit(solution)/shard_map/all_gather | solution.py:191
  857.3 263.3 %copy-start.32 = (f32[1024]{0:T(1024)S(1)}, f32[1024]{0:T(1024)}, u32[]{:S(2)}) copy-start(f32[1024]{0:T(1024)} %param.15) | copy-start | bytes 12292
  857.3 269.8 %slice-start = ((s8[4751360]{0:T(1024)(128)(4,1)}), s8[557056]{0:T(1024)(128)(4,1)S(1)}, s32[]{:S(2)}) async-start(s8[4751360]{0:T(1024)(128)(4,1)} %bitcast.64), calls=%async_computation.15 | async-start | bytes 1114112
  1336.3 8.6 copy-start.13
  1344.9 9.2 copy-start.1
  (31 other events, 145.4 us)
Sparse Core Ops, SparseCore 0:
  119.4 122.6 all-reduce.6
  298.8 119.9 all-reduce.8
  441.4 61.8 reduce-scatter.6
  553.7 85.1 reduce-scatter.4
  643.4 102.5 reduce-scatter.8
  750.6 103.0 reduce-scatter.10
  855.8 41.3 all-gather.6
  899.8 220.8 all-reduce.10
  1122.8 63.2 all-gather.4
  1188.1 73.0 all-gather.8
  1263.4 72.8 all-gather.10
where the time goes:
time: 1370 us; the launch traced here: 1360 us
  waiting for transfers between devices  829 us (61%)
  matrix products  216 us (16%)
  local copies, waits for them, and re-layouts  137 us (10%)
  blocking collectives  103 us (8%)
  other arithmetic  60.6 us (4%)
  between operations  14.6 us (1%)
    psum x1, waiting for transfers between devices, on_device(): lax.psum(jnp.dot(activated, shrink_weight, preferred_element_type=jnp.flo...  195 us
    psum x1, waiting for transfers between devices, on_device(): layer_two_grad = lax.psum(partial_two, 'tensor')  120 us
    psum x1, waiting for transfers between devices, on_device(): lax.psum(jnp.dot(attended, mixing_weight, preferred_element_type=jnp.floa...  110 us
    reduce_scatter x1, waiting for transfers between devices, on_device(): lax.psum_scatter(shrink_grad, 'dp', scatter_dimension=0, tiled=True)  108 us
    reduce_scatter x1, waiting for transfers between devices, on_device(): lax.psum_scatter(expand_grad, 'dp', scatter_dimension=0, tiled=True)  107 us
    all_gather x1, waiting for transfers between devices, on_device(): lax.all_gather(weight_part[3], 'dp', axis=0, tiled=True)  75.1 us
    all_gather x1, waiting for transfers between devices, on_device(): lax.all_gather(weight_part[2], 'dp', axis=0, tiled=True)  69 us
    psum x1, blocking collectives, on_device(): lax.psum((heads_bias_grad, expand_bias_grad), 'dp')  60.9 us
  transfers between devices with their start and end apart: 11, of which 8 were waited for; matrix products, arithmetic and copies ran while one was open for 15% of the time, Pallas kernels for 0%

commit v1 on v0

--- a/solution.py
+++ b/solution.py
@@ -114,7 +114,7 @@
     partial_two = back_dot(pre_low, expand_weight)
     second_scale_part = jnp.sum(partial_two * normed_two, axis=0)
     second_shift_part = jnp.sum(partial_two, axis=0)
-    layer_two_grad = lax.psum(partial_two, "tensor")
+    layer_two_grad = jnp.sum(lax.all_gather(partial_two, "tensor"), axis=0)
     hidden_grad = upstream_wide + norm_back(layer_two_grad, second_scale, normed_two, inverse_two)
     mixing_bias_part = own_sum(hidden_grad)
     hidden_low = hidden_grad.astype(jnp.bfloat16)

time: 1370 us -> 1310 us (0.956)
  waiting for transfers between devices: 829 us -> 767 us
    psum x1 -> x0, waiting for transfers between devices: 120 us -> none  [on_device(): layer_two_grad = lax.psum(partial_two, 'tensor')]
    all_gather x0 -> x1, waiting for transfers between devices: none -> 119 us  [on_device(): layer_two_grad = jnp.sum(lax.all_gather(partial_two, 'tensor'), axis=0)]
    reduce_scatter x1, waiting for transfers between devices: 107 us -> 4.49 us  [on_device(): lax.psum_scatter(expand_grad, 'dp', scatter_dimension=0, tiled=True)]
    all_gather x1, waiting for transfers between devices: 69 us -> 4.84 us  [on_device(): lax.all_gather(weight_part[2], 'dp', axis=0, tiled=True)]
    all_gather x1, waiting for transfers between devices: 0.01 us -> 62.3 us  [on_device(): lax.all_gather(weight_part[0], 'dp', axis=0, tiled=True)]
    reduce_scatter x1, waiting for transfers between devices: 44 us -> 89 us  [on_device(): lax.psum_scatter(heads_grad, 'dp', scatter_dimension=0, tiled=True)]
    unnamed x114 -> x102, local copies, waits for them, and re-layouts: 44 us -> 46 us
  transfers between devices with their start and end apart: 11 -> 11, of which waited for: 8 -> 9; matrix products, arithmetic and copies ran while one was open for 15% -> 16% of each run, Pallas kernels for 0% -> 0%
where the time goes in v1:
time: 1310 us
  waiting for transfers between devices  767 us (59%)
  matrix products  218 us (17%)
  local copies, waits for them, and re-layouts  140 us (11%)
  blocking collectives  103 us (8%)
  other arithmetic  65.9 us (5%)
  between operations  14.6 us (1%)
    psum x1, waiting for transfers between devices, on_device(): lax.psum(jnp.dot(activated, shrink_weight, preferred_element_type=jnp.flo...  194 us
    all_gather x1, waiting for transfers between devices, on_device(): layer_two_grad = jnp.sum(lax.all_gather(partial_two, 'tensor'), axis=0)  119 us
    psum x1, waiting for transfers between devices, on_device(): lax.psum(jnp.dot(attended, mixing_weight, preferred_element_type=jnp.floa...  110 us
    reduce_scatter x1, waiting for transfers between devices, on_device(): lax.psum_scatter(shrink_grad, 'dp', scatter_dimension=0, tiled=True)  108 us
    reduce_scatter x1, waiting for transfers between devices, on_device(): lax.psum_scatter(heads_grad, 'dp', scatter_dimension=0, tiled=True)  89 us
    all_gather x1, waiting for transfers between devices, on_device(): lax.all_gather(weight_part[3], 'dp', axis=0, tiled=True)  75.1 us
    all_gather x1, waiting for transfers between devices, on_device(): lax.all_gather(weight_part[0], 'dp', axis=0, tiled=True)  62.3 us
    psum x1, blocking collectives, on_device(): lax.psum((heads_bias_grad, expand_bias_grad), 'dp')  59.3 us
  transfers between devices with their start and end apart: 11, of which 9 were waited for; matrix products, arithmetic and copies ran while one was open for 16% of the time, Pallas kernels for 0%

profile of v1, /device:TPU:0, one launch (start us, length us, event | category | flops | bytes accessed | tf_op | source)
XLA Modules:
  0.0 1308.8 jit_solution(16055191922737678301)
XLA Ops:
  30.1 6.5 fusion.29
  45.1 5.0 copy.118
  58.5 14.0 %multiply_reduce_fusion.1 = (f32[2,8,577]{2,1,0:T(8,128)S(1)}, f32[2,8,577,577]{2,3,1,0:T(8,128)}) fusion(bf16[2,577,8,64]{1,3,2,0:T(8,128)(2,1)} %copy.120, f32[2,577,8,64]{1,3,2,0:T(8,128)} %copy.118, f32[8,64]{1,0:T(8,128)S(1)} %add.148), kind=kOutput, calls=%fused_computation.6 | convolution fusion | flops 693664768 | bytes 24891520 | tf_op jit(solution)/shard_map/bqhd,bkhd->bhqk/dot_general | solution.py:76
  72.5 10.4 exponential_reduce_fusion
  94.6 12.8 fusion.48
  131.9 110.1 %all-reduce.6.cloned.1.call-done = f32[1154,1024]{1,0:T(8,128)} async-done(((f32[1154,1024]{1,0:T(8,128)}), f32[1154,1024]{1,0:T(8,128)}) %all-reduce.6.cloned.1.call-update) | async-done | bytes 4726800 | tf_op jit(solution)/shard_map/psum | solution.py:85
  250.4 28.1 %fusion.7 = (bf16[1154,2048]{1,0:T(8,128)(2,1)}, f32[1154,2048]{1,0:T(8,128)}) fusion(f32[2048]{0:T(1024)S(1)} %copy-done.37, bf16[1024,2048]{1,0:T(8,128)(2,1)S(1)} %copy-done.35, f32[1154,1024]{1,0:T(8,128)S(1)} %get-tuple-element.91, f32[1024]{0:T(1024)S(1)} %copy-done.38, f32[1024]{0:T(1024)S(1)} %copy-done.29, f32[1154]{0:T(1024)S(1)} %add_rsqrt_fusion.1, ...), kind=kOutput, calls=%fused_computation.14 | convolution fusion | flops 5002119168 | bytes 23127056 | tf_op jit(solution)/shard_map/dot_general | solution.py:89
  278.5 10.9 fusion.69
  289.4 6.8 fusion.33
  296.3 118.8 %all-gather.16.cloned.1.call-done = f32[2,1154,1024]{2,1,0:T(8,128)} async-done(((f32[1,1154,1024]{2,1,0:T(8,128)}), f32[2,1154,1024]{2,1,0:T(8,128)}) %all-gather.16.cloned.1.call-update) | async-done | bytes 9453584 | tf_op jit(solution)/shard_map/all_gather | solution.py:117
  415.1 7.4 reduce_sum.185
  422.5 6.6 multiply_reduce_fusion.3
  437.8 11.4 fusion.31
  451.0 10.4 fusion.73
  472.2 13.3 %fusion.72 = f32[2,8,577,577]{2,3,1,0:T(8,128)} fusion(bf16[2,577,8,64]{1,3,2,0:T(8,128)(2,1)} %copy.125, bf16[2,577,8,64]{1,3,2,0:T(8,128)(2,1)S(1)} %copy-done.7), kind=kOutput, calls=%fused_computation.107 | convolution fusion | flops 681838592 | bytes 23670848 | tf_op jit(solution)/shard_map/bqhd,bkhd->bhqk/dot_general | solution.py:134
  485.5 26.9 %fusion.66 = (f32[8,64]{1,0:T(8,128)S(1)}, bf16[2,577,8,64]{1,3,2,0:T(8,128)(2,1)}) fusion(bf16[2,577,8,64]{1,3,2,0:T(8,128)(2,1)} %copy.120, f32[2,8,577,577]{2,3,1,0:T(8,128)} %fusion.72, f32[2,8,577]{2,1,0:T(8,128)S(1)} %copy-done.24, f32[2,8,577,577]{2,3,1,0:T(8,128)} %get-tuple-element.95, bf16[2,577,8,64]{1,3,2,0:T(8,128)(2,1)} %copy.125, ...), kind=kOutput, calls=%fused_computation.103 | convolution fusion | flops 1412809728 | bytes 47380672 | tf_op jit(solution)/shard_map/bhqk,bkhd->bqhd/dot_general | solution.py:139
  520.9 28.8 %fusion.39 = bf16[2,577,8,64]{1,3,2,0:T(8,128)(2,1)} fusion(f32[2,8,577,577]{2,3,1,0:T(8,128)} %fusion.72, f32[2,8,577]{2,1,0:T(8,128)S(1)} %copy-done.24, f32[2,8,577,577]{2,3,1,0:T(8,128)} %get-tuple-element.95, bf16[2,577,8,64]{1,3,2,0:T(8,128)(2,1)} %copy.125, bf16[2,577,8,64]{1,3,2,0:T(8,128)(2,1)S(1)} %copy-done.7, f32[2,577,8,64]{1,3,2,0:T(8,128)} %copy.118, ...), kind=kOutput, calls=%fused_computation.72 | convolution fusion | flops 1412810240 | bytes 48562368 | tf_op jit(solution)/shard_map/bhqk,bqhd->bkhd/dot_general | solution.py:142
  558.3 11.4 fusion.65
  575.7 9.7 fusion.27
  586.3 10.1 fusion.71
  596.4 5.7 convolution_bitcast_fusion
  606.7 107.5 %reduce-scatter.11.cloned.1.call-done = f32[128,1024]{1,0:T(8,128)} async-done(((f32[2048,1024]{1,0:T(8,128)}), f32[128,1024]{1,0:T(8,128)}) %reduce-scatter.11.cloned.1.call-update) | async-done | bytes 524304 | tf_op jit(solution)/shard_map/reduce_scatter | solution.py:185
  714.3 89.0 %reduce-scatter.5.cloned.1.call-done = f32[64,3,512]{2,0,1:T(8,128)} async-done(((f32[1024,3,512]{2,0,1:T(8,128)}), f32[64,3,512]{2,0,1:T(8,128)}) %reduce-scatter.5.cloned.1.call-update) | async-done | bytes 393232 | tf_op jit(solution)/shard_map/reduce_scatter | solution.py:182
  808.9 5.1 reshape.211
  814.2 59.3 %all-reduce.1 = (f32[2,512]{1,0:T(2,128)}, f32[2048]{0:T(1024)}) all-reduce(f32[2,512]{1,0:T(2,128)S(1)} %pad_maximum_fusion, f32[2048]{0:T(1024)S(1)} %copy-done.30), channel_id=1, replica_groups=mesh['dp'=16,'tensor'=2] {'dp'}, use_global_device_ids=true, to_apply=%region_18.0 | all-reduce | flops 3072 | bytes 24576 | tf_op jit(solution)/shard_map/psum | solution.py:162
  875.4 194.0 %all-reduce.8.cloned.1.call-done = (f32[1154,1024]{1,0:T(8,128)}, f32[1154,1024]{1,0:T(8,128)}) async-done(((f32[1154,1024]{1,0:T(8,128)}, f32[1154,1024]{1,0:T(8,128)}), (f32[1154,1024]{1,0:T(8,128)}, f32[1154,1024]{1,0:T(8,128)})) %all-reduce.8.cloned.1.call-update) | async-done | bytes 9453584 | tf_op jit(solution)/shard_map/psum | solution.py:91
  1069.5 6.4 multiply_reduce_fusion.2
  1087.6 5.0 add_convert_fusion.1
  1098.6 43.5 %all-reduce = (f32[1024]{0:T(1024)}, f32[1024]{0:T(1024)}, f32[1024]{0:T(1024)}, f32[1024]{0:T(1024)}, f32[1024]{0:T(1024)}, /*index=5*/f32[1024]{0:T(1024)}) all-reduce(f32[1024]{0:T(1024)S(1)} %dynamic-slice_reduce_fusion, f32[1024]{0:T(1024)S(1)} %get-tuple-element.72, ...), channel_id=1, replica_groups=mesh['dp'=16,'tensor'=2] {'dp','tensor'}, use_global_device_ids=true, to_apply=%region_21.0 | all-reduce | flops 6144 | bytes 49152 | tf_op jit(solution)/shard_map/psum | solution.py:170
  1146.9 75.1 %all-gather.14.cloned.1.call-done = f32[2048,1024]{1,0:T(8,128)} async-done(((f32[128,1024]{1,0:T(8,128)}), f32[2048,1024]{1,0:T(8,128)}) %all-gather.14.cloned.1.call-update) | async-done | bytes 8388624 | tf_op jit(solution)/shard_map/all_gather | solution.py:191
  1222.0 62.3 %all-gather.8.cloned.1.call-done = f32[1024,3,512]{2,0,1:T(8,128)} async-done(((f32[64,3,512]{2,0,1:T(8,128)}), f32[1024,3,512]{2,0,1:T(8,128)}) %all-gather.8.cloned.1.call-update) | async-done | bytes 6291472 | tf_op jit(solution)/shard_map/all_gather | solution.py:188
  1284.3 6.9 copy.171
  (184 shorter events, 174.8 us)
Async XLA Ops:
  7.2 107.1 %copy-start = (bf16[512,1024]{1,0:T(8,128)(2,1)S(1)}, bf16[512,1024]{1,0:T(8,128)(2,1)}, u32[]{:S(2)}) copy-start(bf16[512,1024]{1,0:T(8,128)(2,1)} %param.19) | copy-start | bytes 3145732
  7.2 234.8 %all-reduce.6.cloned.1.call-start = ((), (), s32[]{:S(2)}) async-start(), calls=%async_computation.4 | async-start | bytes 9502720 | tf_op jit(solution)/shard_map/psum | solution.py:85
  58.5 14.0 %copy-start.25 = (f32[8,64]{1,0:T(8,128)}, f32[8,64]{1,0:T(8,128)S(1)}, u32[]{:S(2)}) copy-start(f32[8,64]{1,0:T(8,128)S(1)} %add.148) | copy-start | bytes 6148
  83.0 11.6 copy-start.23
  94.6 12.8 copy-start.6
  119.2 295.9 %all-gather.16.cloned.1.call-start = ((), (), s32[]{:S(2)}) async-start(), calls=%async_computation.13 | async-start | bytes 14254080 | tf_op jit(solution)/shard_map/all_gather | solution.py:117
  127.3 114.8 %copy-start.31 = (f32[1024]{0:T(1024)S(1)}, f32[1024]{0:T(1024)}, u32[]{:S(2)}) copy-start(f32[1024]{0:T(1024)} %param.20) | copy-start | bytes 12292
  246.4 32.0 %copy-start.1 = (f32[1154,1024]{1,0:T(8,128)}, f32[1154,1024]{1,0:T(8,128)S(1)}, u32[]{:S(2)}) copy-start(f32[1154,1024]{1,0:T(8,128)S(1)} %get-tuple-element.91) | copy-start | bytes 14180356
  250.4 28.1 %copy-start.9 = (bf16[1154,1024]{1,0:T(8,128)(2,1)S(1)}, bf16[1154,1024]{1,0:T(8,128)(2,1)}, u32[]{:S(2)}) copy-start(bf16[1154,1024]{1,0:T(8,128)(2,1)} %reshape.208) | copy-start | bytes 7090180
  250.4 28.1 %copy-start.36 = (bf16[2048,1024]{1,0:T(8,128)(2,1)S(1)}, bf16[2048,1024]{1,0:T(8,128)(2,1)}, u32[]{:S(2)}) copy-start(bf16[2048,1024]{1,0:T(8,128)(2,1)} %param.25) | copy-start | bytes 12582916
  296.2 289.3 %reduce-scatter.7.cloned.1.call-start = ((), (), s32[]{:S(2)}) async-start(), calls=%async_computation.7 | async-start | bytes 2228224 | tf_op jit(solution)/shard_map/reduce_scatter | solution.py:183
  415.1 14.0 %slice-start = ((s8[4751360]{0:T(1024)(128)(4,1)}), s8[557056]{0:T(1024)(128)(4,1)S(1)}, s32[]{:S(2)}) async-start(s8[4751360]{0:T(1024)(128)(4,1)} %bitcast.65), calls=%async_computation.15 | async-start | bytes 1114112
  422.5 8.4 copy-start.10
  437.8 168.9 %reduce-scatter.9.cloned.1.call-start = ((), (), s32[]{:S(2)}) async-start(), calls=%async_computation.9 | async-start | bytes 8912896 | tf_op jit(solution)/shard_map/reduce_scatter | solution.py:184
  449.3 265.0 %reduce-scatter.11.cloned.1.call-start = ((), (), s32[]{:S(2)}) async-start(), calls=%async_computation.11 | async-start | bytes 8912896 | tf_op jit(solution)/shard_map/reduce_scatter | solution.py:185
  461.5 341.9 %reduce-scatter.5.cloned.1.call-start = ((), (), s32[]{:S(2)}) async-start(), calls=%async_computation.5 | async-start | bytes 6684672 | tf_op jit(solution)/shard_map/reduce_scatter | solution.py:182
  472.2 13.3 %copy-start.24 = (f32[2,8,577]{2,1,0:T(8,128)S(1)}, f32[2,8,577]{2,1,0:T(8,128)}, u32[]{:S(2)}) copy-start(f32[2,8,577]{2,1,0:T(8,128)} %copy-done.23) | copy-start | bytes 110788
  512.4 8.5 copy-start.26
  549.7 8.7 copy-start.8
  585.5 290.0 %all-gather.10.cloned.1.call-start = ((), (), s32[]{:S(2)}) async-start(), calls=%async_computation.8 | async-start | bytes 2228224 | tf_op jit(solution)/shard_map/all_gather | solution.py:189
  586.2 10.2 copy-start.20
  586.2 10.2 copy-start.21
  586.2 483.2 %all-reduce.8.cloned.1.call-start = ((), (), s32[]{:S(2)}) async-start(), calls=%async_computation.14 | async-start | bytes 19005440 | tf_op jit(solution)/shard_map/psum | solution.py:91
  586.3 10.1 copy-start.17
  586.3 10.1 copy-start.22
  602.1 203.7 %copy-start.12 = (bf16[2,577,1024]{2,0,1:T(2,128)(2,1)S(1)}, bf16[2,577,1024]{2,0,1:T(2,128)(2,1)}, u32[]{:S(2)}) copy-start(bf16[2,577,1024]{2,0,1:T(2,128)(2,1)} %param.27) | copy-start | bytes 7090180
  602.1 544.8 %all-gather.12.cloned.1.call-start = ((), (), s32[]{:S(2)}) async-start(), calls=%async_computation.10 | async-start | bytes 8912896 | tf_op jit(solution)/shard_map/all_gather | solution.py:190
  606.7 615.3 %all-gather.14.cloned.1.call-start = ((), (), s32[]{:S(2)}) async-start(), calls=%async_computation.12 | async-start | bytes 8912896 | tf_op jit(solution)/shard_map/all_gather | solution.py:191
  714.3 570.0 %all-gather.8.cloned.1.call-start = ((), (), s32[]{:S(2)}) async-start(), calls=%async_computation.6 | async-start | bytes 6684672 | tf_op jit(solution)/shard_map/all_gather | solution.py:188
  808.9 260.6 %copy-start.28 = (f32[1024]{0:T(1024)S(1)}, f32[1024]{0:T(1024)}, u32[]{:S(2)}) copy-start(f32[1024]{0:T(1024)} %param.15) | copy-start | bytes 12292
  808.9 267.0 %slice-start.2 = ((s8[4751360]{0:T(1024)(128)(4,1)}), s8[557056]{0:T(1024)(128)(4,1)S(1)}, s32[]{:S(2)}) async-start(s8[4751360]{0:T(1024)(128)(4,1)} %bitcast.67), calls=%async_computation.17 | async-start | bytes 1114112
  1284.3 8.6 copy-start.13
  (25 other events, 128.1 us)
Sparse Core Ops, SparseCore 0:
  119.3 122.6 all-reduce.5
  296.3 118.6 all-gather.15
  437.9 61.7 reduce-scatter.6
  504.2 102.3 reduce-scatter.8
  611.1 103.0 reduce-scatter.10
  718.6 84.6 reduce-scatter.4
  805.5 40.7 all-gather.9
  848.8 220.6 all-reduce.7
  1071.6 75.2 all-gather.11
  1148.9 73.0 all-gather.13
  1224.2 60.0 all-gather.7
